TPU v7x, 32 devices: a whole 2x2x4 slice. The times are simulated.
32 devices in a mesh: dp: 4 (over x, core), pipe: 2 (over y), tensor: 4 (over z).
Axes of the slice: x: 2, y: 2, z: 4, core: 2. Of those that a mesh axis runs over, the one named last changes fastest.
Arguments:
- weights: bfloat16 [2816, 1408], P(('dp', 'pipe', 'tensor')), may hold values from -6 to 6
- first_moment: bfloat16 [2816, 1408], P(('dp', 'pipe', 'tensor')), may hold values from -6 to 6
- second_moment: bfloat16 [2816, 1408], P(('dp', 'pipe', 'tensor')), may hold values from 0.049804688 to 5
- row_weight: float32 [1408], replicated, may hold values from -1 to 1
- col_weight: float32 [1408], replicated, may hold values from 1 to 4
Outputs:
- weight_tiles: bfloat16 [2816, 1408], P(('pipe', 'tensor'))
- first_tiles: bfloat16 [2816, 1408], P(('pipe', 'tensor'))
- second_tiles: bfloat16 [2816, 1408], P(('pipe', 'tensor'))
- checksums: float32 [3, 2, 4, 11], P(None, 'pipe', 'tensor')
All inputs are finite; a program needn't handle non-finite values.
Results may differ from a plain program's by a relative error of at most 0.001.
Values may be sent and summed in bfloat16 or wider, within the bound.
A program may use at most 64 MiB of HBM per device.

v0:
```python
import jax
import jax.numpy as jnp
from jax import lax
from jax.sharding import PartitionSpec as P

CHECK_COLS = 128


def for_sending(array):
    return jax.tree.map(lambda a: a.astype(jnp.bfloat16) if a.dtype == jnp.float32 else a, array)


def column_sums(data, row_part, col_weight, col_blocks):
    row_mixed = jnp.dot(
        row_part[None, :], data.astype(jnp.float32), precision=lax.Precision.HIGHEST
    )[0]
    return jnp.sum((row_mixed * col_weight).reshape(col_blocks, -1), axis=1)


def shards(weights, first_moment, second_moment, row_weight, col_weight):
    dp_count = lax.axis_size("dp")
    pipe_count = lax.axis_size("pipe")
    tensor_count = lax.axis_size("tensor")
    shard_rows, width = weights.shape
    dp_section = dp_count // pipe_count
    tile_shards = dp_count // tensor_count
    piece_cols = width // dp_count
    tile_rows = shard_rows * dp_count
    col_blocks = width // CHECK_COLS
    factor = float(tile_rows * CHECK_COLS) ** (-0.5)
    sources = (weights, first_moment, second_moment)
    exchanged = (
        lax.all_to_all(sources[0], "dp", split_axis=1, concat_axis=0, tiled=True),
        lax.all_to_all(sources[1], "dp", split_axis=1, concat_axis=0, tiled=True),
        lax.all_to_all(sources[2], "dp", split_axis=1, concat_axis=0, tiled=True),
    )
    grouped = tuple(
        (item.reshape(pipe_count, dp_section, shard_rows, piece_cols) for item in exchanged)
    )
    sectioned = jax.tree.map(
        lambda part, own: part.astype(own.dtype),
        lax.all_to_all(for_sending(grouped), "pipe", split_axis=0, concat_axis=2, tiled=True),
        grouped,
    )
    routed = tuple(
        (item.reshape(tensor_count, tile_shards, 1, shard_rows, piece_cols) for item in sectioned)
    )
    arrived = jax.tree.map(
        lambda part, own: part.astype(own.dtype),
        lax.all_to_all(for_sending(routed), "tensor", split_axis=0, concat_axis=2, tiled=True),
        routed,
    )
    flat_pieces = tuple((item.reshape(tile_rows, piece_cols) for item in arrived))
    tiles = jax.tree.map(
        lambda part, own: part.astype(own.dtype),
        lax.all_gather(for_sending(flat_pieces), "dp", axis=1, tiled=True),
        flat_pieces,
    )
    tensor_pos = lax.axis_index("tensor")
    flat_index = (
        lax.axis_index("dp") * pipe_count + lax.axis_index("pipe")
    ) * tensor_count + tensor_pos
    in_section = flat_index % (dp_count * tensor_count)
    section_of = flat_index // (dp_count * tensor_count)
    tile_of = in_section // dp_count
    row_part = lax.dynamic_slice_in_dim(row_weight, in_section * shard_rows, shard_rows)
    partial_value = jnp.stack(
        [column_sums(item, row_part, col_weight, col_blocks) for item in sources]
    )
    section_hit = (jnp.arange(pipe_count) == section_of).astype(jnp.float32)
    tile_hit = (jnp.arange(tensor_count) == tile_of).astype(jnp.float32)
    spread = (
        partial_value[:, None, None, :]
        * section_hit[None, :, None, None]
        * tile_hit[None, None, :, None]
    )
    summed = lax.psum(spread, ("dp", "pipe", "tensor"))
    checks = (
        lax.dynamic_slice(summed, (0, lax.axis_index("pipe"), tensor_pos, 0), (3, 1, 1, col_blocks))
        * factor
    )
    return (tiles[0], tiles[1], tiles[2], checks)


def solution(mesh):
    return jax.shard_map(
        shards,
        mesh=mesh,
        in_specs=(
            P(("dp", "pipe", "tensor"), None),
            P(("dp", "pipe", "tensor"), None),
            P(("dp", "pipe", "tensor"), None),
            P(),
            P(),
        ),
        out_specs=(
            P(("pipe", "tensor"), None),
            P(("pipe", "tensor"), None),
            P(("pipe", "tensor"), None),
            P(None, "pipe", "tensor", None),
        ),
        check_vma=False,
    )
```

profile of v0, /device:TPU:0, one launch (start us, length us, event | category | flops | bytes accessed | tf_op | source)
XLA Modules:
  0.0 154.1 jit_solution(8427268718347811385)
XLA Ops:
  0.7 1.3 all_to_all.90
  1.9 0.7 copy.33
  2.7 4.4 %all-to-all-start = ((bf16[88,4,352]{2,0,1:T(8,128)(2,1)}), bf16[88,4,352]{2,0,1:T(8,128)(2,1)}, u32[]{:S(2)}, u32[]{:S(2)}) async-start(bf16[88,4,352]{2,0,1:T(8,128)(2,1)} %copy.33), calls=%async_computation | async-start | bytes 540672 | tf_op jit(solution)/shard_map/all_to_all | solution.py:33
  8.1 5.6 %all-to-all-done = bf16[88,4,352]{2,0,1:T(8,128)(2,1)} async-done(((bf16[88,4,352]{2,0,1:T(8,128)(2,1)}), bf16[88,4,352]{2,0,1:T(8,128)(2,1)}, u32[]{:S(2)}, u32[]{:S(2)}) %all-to-all-start) | async-done | bytes 247840 | tf_op jit(solution)/shard_map/all_to_all | solution.py:33
  13.7 4.1 %all-to-all-start.3 = ((bf16[88,4,352]{2,0,1:T(8,128)(2,1)}), bf16[88,4,352]{2,0,1:T(8,128)(2,1)}, u32[]{:S(2)}, u32[]{:S(2)}) async-start(bf16[88,4,352]{2,0,1:T(8,128)(2,1)} %copy.37), calls=%async_computation.3 | async-start | bytes 540672 | tf_op jit(solution)/shard_map/all_to_all | solution.py:34
  18.9 5.1 %all-to-all-done.3 = bf16[88,4,352]{2,0,1:T(8,128)(2,1)} async-done(((bf16[88,4,352]{2,0,1:T(8,128)(2,1)}), bf16[88,4,352]{2,0,1:T(8,128)(2,1)}, u32[]{:S(2)}, u32[]{:S(2)}) %all-to-all-start.3) | async-done | bytes 247840 | tf_op jit(solution)/shard_map/all_to_all | solution.py:34
  24.0 4.1 %all-to-all-start.6 = ((bf16[88,4,352]{2,0,1:T(8,128)(2,1)}), bf16[88,4,352]{2,0,1:T(8,128)(2,1)}, u32[]{:S(2)}, u32[]{:S(2)}) async-start(bf16[88,4,352]{2,0,1:T(8,128)(2,1)} %copy.41), calls=%async_computation.6 | async-start | bytes 540672 | tf_op jit(solution)/shard_map/all_to_all | solution.py:35
  28.7 5.5 %all-to-all-done.6 = bf16[88,4,352]{2,0,1:T(8,128)(2,1)} async-done(((bf16[88,4,352]{2,0,1:T(8,128)(2,1)}), bf16[88,4,352]{2,0,1:T(8,128)(2,1)}, u32[]{:S(2)}, u32[]{:S(2)}) %all-to-all-start.6) | async-done | bytes 247840 | tf_op jit(solution)/shard_map/all_to_all | solution.py:35
  34.2 3.6 %all-to-all-start.1 = ((bf16[2,2,88,352]{3,2,1,0:T(8,128)(2,1)}), bf16[2,2,88,352]{3,2,1,0:T(8,128)(2,1)S(1)}, u32[]{:S(2)}, u32[]{:S(2)}) async-start(bf16[2,2,88,352]{3,2,1,0:T(8,128)(2,1)} %bitcast.1), calls=%async_computation.1 | async-start | bytes 540672 | tf_op jit(solution)/shard_map/all_to_all | solution.py:42
  38.3 5.2 %all-to-all-done.1 = bf16[2,2,88,352]{3,2,1,0:T(8,128)(2,1)S(1)} async-done(((bf16[2,2,88,352]{3,2,1,0:T(8,128)(2,1)}), bf16[2,2,88,352]{3,2,1,0:T(8,128)(2,1)S(1)}, u32[]{:S(2)}, u32[]{:S(2)}) %all-to-all-start.1) | async-done | bytes 247840 | tf_op jit(solution)/shard_map/all_to_all | solution.py:42
  43.5 3.4 %all-to-all-start.4 = ((bf16[2,2,88,352]{3,2,1,0:T(8,128)(2,1)}), bf16[2,2,88,352]{3,2,1,0:T(8,128)(2,1)S(1)}, u32[]{:S(2)}, u32[]{:S(2)}) async-start(bf16[2,2,88,352]{3,2,1,0:T(8,128)(2,1)} %bitcast.8), calls=%async_computation.4 | async-start | bytes 540672 | tf_op jit(solution)/shard_map/all_to_all | solution.py:42
  47.0 5.2 %all-to-all-done.4 = bf16[2,2,88,352]{3,2,1,0:T(8,128)(2,1)S(1)} async-done(((bf16[2,2,88,352]{3,2,1,0:T(8,128)(2,1)}), bf16[2,2,88,352]{3,2,1,0:T(8,128)(2,1)S(1)}, u32[]{:S(2)}, u32[]{:S(2)}) %all-to-all-start.4) | async-done | bytes 247840 | tf_op jit(solution)/shard_map/all_to_all | solution.py:42
  52.1 3.4 %all-to-all-start.7 = ((bf16[2,2,88,352]{3,2,1,0:T(8,128)(2,1)}), bf16[2,2,88,352]{3,2,1,0:T(8,128)(2,1)S(1)}, u32[]{:S(2)}, u32[]{:S(2)}) async-start(bf16[2,2,88,352]{3,2,1,0:T(8,128)(2,1)} %bitcast.15), calls=%async_computation.7 | async-start | bytes 540672 | tf_op jit(solution)/shard_map/all_to_all | solution.py:42
  56.4 4.4 %all-to-all-done.7 = bf16[2,2,88,352]{3,2,1,0:T(8,128)(2,1)S(1)} async-done(((bf16[2,2,88,352]{3,2,1,0:T(8,128)(2,1)}), bf16[2,2,88,352]{3,2,1,0:T(8,128)(2,1)S(1)}, u32[]{:S(2)}, u32[]{:S(2)}) %all-to-all-start.7) | async-done | bytes 247840 | tf_op jit(solution)/shard_map/all_to_all | solution.py:42
  60.8 5.1 %all-to-all-start.2 = ((bf16[4,1,1,88,352]{4,3,2,1,0:T(8,128)(2,1)}), bf16[4,1,1,88,352]{4,3,2,1,0:T(8,128)(2,1)S(1)}, u32[]{:S(2)}, u32[]{:S(2)}) async-start(bf16[4,1,1,88,352]{4,3,2,1,0:T(8,128)(2,1)} %bitcast.5), calls=%async_computation.2 | async-start | bytes 540672 | tf_op jit(solution)/shard_map/all_to_all | solution.py:50
  65.9 39.9 %psum.7 = f32[3,2,4,11]{3,2,1,0:T(4,128)S(1)} all-reduce(f32[3,2,4,11]{3,2,1,0:T(4,128)S(1)} %broadcast_multiply_fusion), channel_id=1, replica_groups=mesh['dp'=4,'pipe'=2,'tensor'=4] {'dp','pipe','tensor'}, use_global_device_ids=true, to_apply=%region_3.4 | all-reduce | flops 264 | bytes 2112 | tf_op jit(solution)/shard_map/psum | solution.py:77
  107.9 3.6 %all-to-all-start.5 = ((bf16[4,1,1,88,352]{4,3,2,1,0:T(8,128)(2,1)}), bf16[4,1,1,88,352]{4,3,2,1,0:T(8,128)(2,1)S(1)}, u32[]{:S(2)}, u32[]{:S(2)}) async-start(bf16[4,1,1,88,352]{4,3,2,1,0:T(8,128)(2,1)} %bitcast.12), calls=%async_computation.5 | async-start | bytes 540672 | tf_op jit(solution)/shard_map/all_to_all | solution.py:50
  111.6 11.0 %all_gather.9 = bf16[352,1408]{0,1:T(8,128)(2,1)S(1)} all-gather(bf16[352,352]{0,1:T(8,128)(2,1)S(1)} %copy.36), channel_id=1, replica_groups=mesh['dp'=4,'pipe'=2,'tensor'=4] {'dp'}, dimensions={1}, use_global_device_ids=true | all-gather | bytes 1239040 | tf_op jit(solution)/shard_map/all_gather | solution.py:56
  122.6 1.9 %copy.45 = bf16[352,1408]{1,0:T(8,128)(2,1)} copy(bf16[352,1408]{0,1:T(8,128)(2,1)S(1)} %all_gather.9) | data formatting | bytes 1982464
  124.5 5.1 %all-to-all-start.8 = ((bf16[4,1,1,88,352]{4,3,2,1,0:T(8,128)(2,1)}), bf16[4,1,1,88,352]{4,3,2,1,0:T(8,128)(2,1)S(1)}, u32[]{:S(2)}, u32[]{:S(2)}) async-start(bf16[4,1,1,88,352]{4,3,2,1,0:T(8,128)(2,1)} %bitcast.19), calls=%async_computation.8 | async-start | bytes 540672 | tf_op jit(solution)/shard_map/all_to_all | solution.py:50
  129.8 10.0 %all_gather.10 = bf16[352,1408]{0,1:T(8,128)(2,1)S(1)} all-gather(bf16[352,352]{0,1:T(8,128)(2,1)S(1)} %copy.40), channel_id=1, replica_groups=mesh['dp'=4,'pipe'=2,'tensor'=4] {'dp'}, dimensions={1}, use_global_device_ids=true | all-gather | bytes 1239040 | tf_op jit(solution)/shard_map/all_gather | solution.py:56
  139.8 1.9 %copy.46 = bf16[352,1408]{1,0:T(8,128)(2,1)} copy(bf16[352,1408]{0,1:T(8,128)(2,1)S(1)} %all_gather.10) | data formatting | bytes 1982464
  141.9 10.3 %all_gather.11 = bf16[352,1408]{0,1:T(8,128)(2,1)S(1)} all-gather(bf16[352,352]{0,1:T(8,128)(2,1)S(1)} %copy.44), channel_id=1, replica_groups=mesh['dp'=4,'pipe'=2,'tensor'=4] {'dp'}, dimensions={1}, use_global_device_ids=true | all-gather | bytes 1239040 | tf_op jit(solution)/shard_map/all_gather | solution.py:56
  152.2 1.9 %copy.47 = bf16[352,1408]{1,0:T(8,128)(2,1)} copy(bf16[352,1408]{0,1:T(8,128)(2,1)S(1)} %all_gather.11) | data formatting | bytes 1982464
  (33 shorter events, 6.7 us)
Async XLA Ops:
  0.6 27.4 %copy-start = (f32[1408]{0:T(1024)S(1)}, f32[1408]{0:T(1024)}, u32[]{:S(2)}) copy-start(f32[1408]{0:T(1024)} %param.8) | copy-start | bytes 16900
  0.6 6.4 %copy-start.3 = (bf16[88,1408]{1,0:T(8,128)(2,1)S(1)}, bf16[88,1408]{1,0:T(8,128)(2,1)}, u32[]{:S(2)}) copy-start(bf16[88,1408]{1,0:T(8,128)(2,1)} %param.6) | copy-start | bytes 743428
  2.7 15.2 %copy-start.2 = (bf16[88,1408]{1,0:T(8,128)(2,1)S(1)}, bf16[88,1408]{1,0:T(8,128)(2,1)}, u32[]{:S(2)}) copy-start(bf16[88,1408]{1,0:T(8,128)(2,1)} %param.7) | copy-start | bytes 743428
  2.7 11.0 %all-to-all-start = ((bf16[88,4,352]{2,0,1:T(8,128)(2,1)}), bf16[88,4,352]{2,0,1:T(8,128)(2,1)}, u32[]{:S(2)}, u32[]{:S(2)}) async-start(bf16[88,4,352]{2,0,1:T(8,128)(2,1)} %copy.33), calls=%async_computation | async-start | bytes 540672 | tf_op jit(solution)/shard_map/all_to_all | solution.py:33
  8.1 20.0 %copy-start.1 = (bf16[88,1408]{1,0:T(8,128)(2,1)S(1)}, bf16[88,1408]{1,0:T(8,128)(2,1)}, u32[]{:S(2)}) copy-start(bf16[88,1408]{1,0:T(8,128)(2,1)} %param.5) | copy-start | bytes 743428
  13.7 10.2 %all-to-all-start.3 = ((bf16[88,4,352]{2,0,1:T(8,128)(2,1)}), bf16[88,4,352]{2,0,1:T(8,128)(2,1)}, u32[]{:S(2)}, u32[]{:S(2)}) async-start(bf16[88,4,352]{2,0,1:T(8,128)(2,1)} %copy.37), calls=%async_computation.3 | async-start | bytes 540672 | tf_op jit(solution)/shard_map/all_to_all | solution.py:34
  18.1 20.0 %copy-start.4 = (f32[1408]{0:T(1024)S(1)}, f32[1408]{0:T(1024)}, u32[]{:S(2)}) copy-start(f32[1408]{0:T(1024)} %param.9) | copy-start | bytes 16900
  24.0 10.2 %all-to-all-start.6 = ((bf16[88,4,352]{2,0,1:T(8,128)(2,1)}), bf16[88,4,352]{2,0,1:T(8,128)(2,1)}, u32[]{:S(2)}, u32[]{:S(2)}) async-start(bf16[88,4,352]{2,0,1:T(8,128)(2,1)} %copy.41), calls=%async_computation.6 | async-start | bytes 540672 | tf_op jit(solution)/shard_map/all_to_all | solution.py:35
  34.2 9.3 %all-to-all-start.1 = ((bf16[2,2,88,352]{3,2,1,0:T(8,128)(2,1)}), bf16[2,2,88,352]{3,2,1,0:T(8,128)(2,1)S(1)}, u32[]{:S(2)}, u32[]{:S(2)}) async-start(bf16[2,2,88,352]{3,2,1,0:T(8,128)(2,1)} %bitcast.1), calls=%async_computation.1 | async-start | bytes 540672 | tf_op jit(solution)/shard_map/all_to_all | solution.py:42
  43.5 8.7 %all-to-all-start.4 = ((bf16[2,2,88,352]{3,2,1,0:T(8,128)(2,1)}), bf16[2,2,88,352]{3,2,1,0:T(8,128)(2,1)S(1)}, u32[]{:S(2)}, u32[]{:S(2)}) async-start(bf16[2,2,88,352]{3,2,1,0:T(8,128)(2,1)} %bitcast.8), calls=%async_computation.4 | async-start | bytes 540672 | tf_op jit(solution)/shard_map/all_to_all | solution.py:42
  52.1 8.7 %all-to-all-start.7 = ((bf16[2,2,88,352]{3,2,1,0:T(8,128)(2,1)}), bf16[2,2,88,352]{3,2,1,0:T(8,128)(2,1)S(1)}, u32[]{:S(2)}, u32[]{:S(2)}) async-start(bf16[2,2,88,352]{3,2,1,0:T(8,128)(2,1)} %bitcast.15), calls=%async_computation.7 | async-start | bytes 540672 | tf_op jit(solution)/shard_map/all_to_all | solution.py:42
  60.8 47.1 %all-to-all-start.2 = ((bf16[4,1,1,88,352]{4,3,2,1,0:T(8,128)(2,1)}), bf16[4,1,1,88,352]{4,3,2,1,0:T(8,128)(2,1)S(1)}, u32[]{:S(2)}, u32[]{:S(2)}) async-start(bf16[4,1,1,88,352]{4,3,2,1,0:T(8,128)(2,1)} %bitcast.5), calls=%async_computation.2 | async-start | bytes 540672 | tf_op jit(solution)/shard_map/all_to_all | solution.py:50
  107.9 16.6 %all-to-all-start.5 = ((bf16[4,1,1,88,352]{4,3,2,1,0:T(8,128)(2,1)}), bf16[4,1,1,88,352]{4,3,2,1,0:T(8,128)(2,1)S(1)}, u32[]{:S(2)}, u32[]{:S(2)}) async-start(bf16[4,1,1,88,352]{4,3,2,1,0:T(8,128)(2,1)} %bitcast.12), calls=%async_computation.5 | async-start | bytes 540672 | tf_op jit(solution)/shard_map/all_to_all | solution.py:50
  124.5 17.2 %all-to-all-start.8 = ((bf16[4,1,1,88,352]{4,3,2,1,0:T(8,128)(2,1)}), bf16[4,1,1,88,352]{4,3,2,1,0:T(8,128)(2,1)S(1)}, u32[]{:S(2)}, u32[]{:S(2)}) async-start(bf16[4,1,1,88,352]{4,3,2,1,0:T(8,128)(2,1)} %bitcast.19), calls=%async_computation.8 | async-start | bytes 540672 | tf_op jit(solution)/shard_map/all_to_all | solution.py:50
where the time goes:
time: 155 us; the launch traced here: 154 us
  blocking collectives  71.2 us (46%)
  starting transfers between devices  36.7 us (24%)
  waiting for transfers between devices  31 us (20%)
  local copies, waits for them, and re-layouts  12.5 us (8%)
    psum x1, blocking collectives, shards(): summed = lax.psum(spread, ('dp', 'pipe', 'tensor'))  39.9 us
    all_gather x3, blocking collectives, shards(): lax.all_gather(for_sending(flat_pieces), 'dp', axis=1, tiled=True)  31.3 us
    all_to_all x3, waiting for transfers between devices, shards(): lax.all_to_all(for_sending(grouped), 'pipe', split_axis=0, concat_axis=2,...  14.7 us
    all_to_all x3, starting transfers between devices, shards(): lax.all_to_all(for_sending(routed), 'tensor', split_axis=0, concat_axis=2...  13.7 us
    all_to_all x3, starting transfers between devices, shards(): lax.all_to_all(for_sending(grouped), 'pipe', split_axis=0, concat_axis=2,...  10.5 us
    unnamed x13, local copies, waits for them, and re-layouts  5.65 us
    all_to_all x1, waiting for transfers between devices, shards(): lax.all_to_all(sources[0], 'dp', split_axis=1, concat_axis=0, tiled=True)  5.65 us
    all_to_all x1, waiting for transfers between devices, shards(): lax.all_to_all(sources[2], 'dp', split_axis=1, concat_axis=0, tiled=True)  5.51 us
  transfers between devices with their start and end apart: 9, of which 6 were waited for; matrix products, arithmetic and copies ran while one was open for 6% of the time, Pallas kernels for 0%

commit v1 on v0

--- a/solution.py
+++ b/solution.py
@@ -74,7 +74,7 @@
         * section_hit[None, :, None, None]
         * tile_hit[None, None, :, None]
     )
-    summed = lax.psum(spread, ("dp", "pipe", "tensor"))
+    summed = lax.psum(lax.psum(spread, ("pipe", "tensor")), "dp")
     checks = (
         lax.dynamic_slice(summed, (0, lax.axis_index("pipe"), tensor_pos, 0), (3, 1, 1, col_blocks))
         * factor

time: 155 us -> 160 us (1.032)
  blocking collectives: 71.2 us -> 76.4 us
    psum x1 -> x2, blocking collectives: 39.9 us -> 46.7 us  [shards(): summed = lax.psum(lax.psum(spread, ('pipe', 'tensor')), 'dp')]
where the time goes in v1:
time: 160 us; the launch traced here: 159 us
  blocking collectives  76.4 us (48%)
  starting transfers between devices  36.6 us (23%)
  waiting for transfers between devices  31 us (19%)
  local copies, waits for them, and re-layouts  12.5 us (8%)
    psum x2, blocking collectives, shards(): summed = lax.psum(lax.psum(spread, ('pipe', 'tensor')), 'dp')  46.7 us
    all_gather x3, blocking collectives, shards(): lax.all_gather(for_sending(flat_pieces), 'dp', axis=1, tiled=True)  29.8 us
    all_to_all x3, waiting for transfers between devices, shards(): lax.all_to_all(for_sending(grouped), 'pipe', split_axis=0, concat_axis=2,...  14.7 us
    all_to_all x3, starting transfers between devices, shards(): lax.all_to_all(for_sending(routed), 'tensor', split_axis=0, concat_axis=2...  13.6 us
    all_to_all x3, starting transfers between devices, shards(): lax.all_to_all(for_sending(grouped), 'pipe', split_axis=0, concat_axis=2,...  10.5 us
    all_to_all x1, waiting for transfers between devices, shards(): lax.all_to_all(sources[0], 'dp', split_axis=1, concat_axis=0, tiled=True)  5.65 us
    unnamed x13, local copies, waits for them, and re-layouts  5.65 us
    all_to_all x1, waiting for transfers between devices, shards(): lax.all_to_all(sources[2], 'dp', split_axis=1, concat_axis=0, tiled=True)  5.51 us
  transfers between devices with their start and end apart: 9, of which 6 were waited for; matrix products, arithmetic and copies ran while one was open for 6% of the time, Pallas kernels for 0%

profile of v1, /device:TPU:0, one launch (start us, length us, event | category | flops | bytes accessed | tf_op | source)
XLA Modules:
  0.0 159.2 jit_solution(11384963092602040313)
XLA Ops:
  0.7 1.3 all_to_all.90
  2.7 4.4 %all-to-all-start = ((bf16[88,4,352]{2,0,1:T(8,128)(2,1)}), bf16[88,4,352]{2,0,1:T(8,128)(2,1)}, u32[]{:S(2)}, u32[]{:S(2)}) async-start(bf16[88,4,352]{2,0,1:T(8,128)(2,1)} %copy.33), calls=%async_computation | async-start | bytes 540672 | tf_op jit(solution)/shard_map/all_to_all | solution.py:33
  8.1 5.7 %all-to-all-done = bf16[88,4,352]{2,0,1:T(8,128)(2,1)} async-done(((bf16[88,4,352]{2,0,1:T(8,128)(2,1)}), bf16[88,4,352]{2,0,1:T(8,128)(2,1)}, u32[]{:S(2)}, u32[]{:S(2)}) %all-to-all-start) | async-done | bytes 247840 | tf_op jit(solution)/shard_map/all_to_all | solution.py:33
  13.7 4.1 %all-to-all-start.3 = ((bf16[88,4,352]{2,0,1:T(8,128)(2,1)}), bf16[88,4,352]{2,0,1:T(8,128)(2,1)}, u32[]{:S(2)}, u32[]{:S(2)}) async-start(bf16[88,4,352]{2,0,1:T(8,128)(2,1)} %copy.37), calls=%async_computation.3 | async-start | bytes 540672 | tf_op jit(solution)/shard_map/all_to_all | solution.py:34
  18.9 5.1 %all-to-all-done.3 = bf16[88,4,352]{2,0,1:T(8,128)(2,1)} async-done(((bf16[88,4,352]{2,0,1:T(8,128)(2,1)}), bf16[88,4,352]{2,0,1:T(8,128)(2,1)}, u32[]{:S(2)}, u32[]{:S(2)}) %all-to-all-start.3) | async-done | bytes 247840 | tf_op jit(solution)/shard_map/all_to_all | solution.py:34
  24.0 4.1 %all-to-all-start.6 = ((bf16[88,4,352]{2,0,1:T(8,128)(2,1)}), bf16[88,4,352]{2,0,1:T(8,128)(2,1)}, u32[]{:S(2)}, u32[]{:S(2)}) async-start(bf16[88,4,352]{2,0,1:T(8,128)(2,1)} %copy.41), calls=%async_computation.6 | async-start | bytes 540672 | tf_op jit(solution)/shard_map/all_to_all | solution.py:35
  28.7 5.5 %all-to-all-done.6 = bf16[88,4,352]{2,0,1:T(8,128)(2,1)} async-done(((bf16[88,4,352]{2,0,1:T(8,128)(2,1)}), bf16[88,4,352]{2,0,1:T(8,128)(2,1)}, u32[]{:S(2)}, u32[]{:S(2)}) %all-to-all-start.6) | async-done | bytes 247840 | tf_op jit(solution)/shard_map/all_to_all | solution.py:35
  34.2 3.6 %all-to-all-start.1 = ((bf16[2,2,88,352]{3,2,1,0:T(8,128)(2,1)}), bf16[2,2,88,352]{3,2,1,0:T(8,128)(2,1)S(1)}, u32[]{:S(2)}, u32[]{:S(2)}) async-start(bf16[2,2,88,352]{3,2,1,0:T(8,128)(2,1)} %bitcast.1), calls=%async_computation.1 | async-start | bytes 540672 | tf_op jit(solution)/shard_map/all_to_all | solution.py:42
  38.3 5.2 %all-to-all-done.1 = bf16[2,2,88,352]{3,2,1,0:T(8,128)(2,1)S(1)} async-done(((bf16[2,2,88,352]{3,2,1,0:T(8,128)(2,1)}), bf16[2,2,88,352]{3,2,1,0:T(8,128)(2,1)S(1)}, u32[]{:S(2)}, u32[]{:S(2)}) %all-to-all-start.1) | async-done | bytes 247840 | tf_op jit(solution)/shard_map/all_to_all | solution.py:42
  43.5 3.4 %all-to-all-start.4 = ((bf16[2,2,88,352]{3,2,1,0:T(8,128)(2,1)}), bf16[2,2,88,352]{3,2,1,0:T(8,128)(2,1)S(1)}, u32[]{:S(2)}, u32[]{:S(2)}) async-start(bf16[2,2,88,352]{3,2,1,0:T(8,128)(2,1)} %bitcast.8), calls=%async_computation.4 | async-start | bytes 540672 | tf_op jit(solution)/shard_map/all_to_all | solution.py:42
  47.0 5.2 %all-to-all-done.4 = bf16[2,2,88,352]{3,2,1,0:T(8,128)(2,1)S(1)} async-done(((bf16[2,2,88,352]{3,2,1,0:T(8,128)(2,1)}), bf16[2,2,88,352]{3,2,1,0:T(8,128)(2,1)S(1)}, u32[]{:S(2)}, u32[]{:S(2)}) %all-to-all-start.4) | async-done | bytes 247840 | tf_op jit(solution)/shard_map/all_to_all | solution.py:42
  52.1 3.4 %all-to-all-start.7 = ((bf16[2,2,88,352]{3,2,1,0:T(8,128)(2,1)}), bf16[2,2,88,352]{3,2,1,0:T(8,128)(2,1)S(1)}, u32[]{:S(2)}, u32[]{:S(2)}) async-start(bf16[2,2,88,352]{3,2,1,0:T(8,128)(2,1)} %bitcast.15), calls=%async_computation.7 | async-start | bytes 540672 | tf_op jit(solution)/shard_map/all_to_all | solution.py:42
  56.4 4.4 %all-to-all-done.7 = bf16[2,2,88,352]{3,2,1,0:T(8,128)(2,1)S(1)} async-done(((bf16[2,2,88,352]{3,2,1,0:T(8,128)(2,1)}), bf16[2,2,88,352]{3,2,1,0:T(8,128)(2,1)S(1)}, u32[]{:S(2)}, u32[]{:S(2)}) %all-to-all-start.7) | async-done | bytes 247840 | tf_op jit(solution)/shard_map/all_to_all | solution.py:42
  60.8 5.1 %all-to-all-start.2 = ((bf16[4,1,1,88,352]{4,3,2,1,0:T(8,128)(2,1)}), bf16[4,1,1,88,352]{4,3,2,1,0:T(8,128)(2,1)S(1)}, u32[]{:S(2)}, u32[]{:S(2)}) async-start(bf16[4,1,1,88,352]{4,3,2,1,0:T(8,128)(2,1)} %bitcast.5), calls=%async_computation.2 | async-start | bytes 540672 | tf_op jit(solution)/shard_map/all_to_all | solution.py:50
  66.0 36.3 %psum.14 = f32[3,2,4,11]{3,2,1,0:T(4,128)S(1)} all-reduce(f32[3,2,4,11]{3,2,1,0:T(4,128)S(1)} %broadcast_multiply_fusion), channel_id=1, replica_groups=mesh['dp'=4,'pipe'=2,'tensor'=4] {'pipe','tensor'}, use_global_device_ids=true, to_apply=%region_3.4 | all-reduce | flops 264 | bytes 2112 | tf_op jit(solution)/shard_map/psum | solution.py:77
  102.2 10.4 %psum.15 = f32[3,2,4,11]{3,2,1,0:T(4,128)S(1)} all-reduce(f32[3,2,4,11]{3,2,1,0:T(4,128)S(1)} %psum.14), channel_id=1, replica_groups=mesh['dp'=4,'pipe'=2,'tensor'=4] {'dp'}, use_global_device_ids=true, to_apply=%region_4.5 | all-reduce | flops 264 | bytes 2112 | tf_op jit(solution)/shard_map/psum | solution.py:77
  114.7 3.5 %all-to-all-start.5 = ((bf16[4,1,1,88,352]{4,3,2,1,0:T(8,128)(2,1)}), bf16[4,1,1,88,352]{4,3,2,1,0:T(8,128)(2,1)S(1)}, u32[]{:S(2)}, u32[]{:S(2)}) async-start(bf16[4,1,1,88,352]{4,3,2,1,0:T(8,128)(2,1)} %bitcast.12), calls=%async_computation.5 | async-start | bytes 540672 | tf_op jit(solution)/shard_map/all_to_all | solution.py:50
  118.4 9.2 %all_gather.9 = bf16[352,1408]{0,1:T(8,128)(2,1)S(1)} all-gather(bf16[352,352]{0,1:T(8,128)(2,1)S(1)} %copy.36), channel_id=1, replica_groups=mesh['dp'=4,'pipe'=2,'tensor'=4] {'dp'}, dimensions={1}, use_global_device_ids=true | all-gather | bytes 1239040 | tf_op jit(solution)/shard_map/all_gather | solution.py:56
  127.6 1.9 %copy.45 = bf16[352,1408]{1,0:T(8,128)(2,1)} copy(bf16[352,1408]{0,1:T(8,128)(2,1)S(1)} %all_gather.9) | data formatting | bytes 1982464
  129.4 5.1 %all-to-all-start.8 = ((bf16[4,1,1,88,352]{4,3,2,1,0:T(8,128)(2,1)}), bf16[4,1,1,88,352]{4,3,2,1,0:T(8,128)(2,1)S(1)}, u32[]{:S(2)}, u32[]{:S(2)}) async-start(bf16[4,1,1,88,352]{4,3,2,1,0:T(8,128)(2,1)} %bitcast.19), calls=%async_computation.8 | async-start | bytes 540672 | tf_op jit(solution)/shard_map/all_to_all | solution.py:50
  134.7 10.2 %all_gather.10 = bf16[352,1408]{0,1:T(8,128)(2,1)S(1)} all-gather(bf16[352,352]{0,1:T(8,128)(2,1)S(1)} %copy.40), channel_id=1, replica_groups=mesh['dp'=4,'pipe'=2,'tensor'=4] {'dp'}, dimensions={1}, use_global_device_ids=true | all-gather | bytes 1239040 | tf_op jit(solution)/shard_map/all_gather | solution.py:56
  144.9 1.9 %copy.46 = bf16[352,1408]{1,0:T(8,128)(2,1)} copy(bf16[352,1408]{0,1:T(8,128)(2,1)S(1)} %all_gather.10) | data formatting | bytes 1982464
  147.0 10.3 %all_gather.11 = bf16[352,1408]{0,1:T(8,128)(2,1)S(1)} all-gather(bf16[352,352]{0,1:T(8,128)(2,1)S(1)} %copy.44), channel_id=1, replica_groups=mesh['dp'=4,'pipe'=2,'tensor'=4] {'dp'}, dimensions={1}, use_global_device_ids=true | all-gather | bytes 1239040 | tf_op jit(solution)/shard_map/all_gather | solution.py:56
  157.3 1.9 %copy.47 = bf16[352,1408]{1,0:T(8,128)(2,1)} copy(bf16[352,1408]{0,1:T(8,128)(2,1)S(1)} %all_gather.11) | data formatting | bytes 1982464
  (34 shorter events, 7.4 us)
Async XLA Ops:
  0.6 27.4 %copy-start = (f32[1408]{0:T(1024)S(1)}, f32[1408]{0:T(1024)}, u32[]{:S(2)}) copy-start(f32[1408]{0:T(1024)} %param.8) | copy-start | bytes 16900
  0.6 6.4 %copy-start.3 = (bf16[88,1408]{1,0:T(8,128)(2,1)S(1)}, bf16[88,1408]{1,0:T(8,128)(2,1)}, u32[]{:S(2)}) copy-start(bf16[88,1408]{1,0:T(8,128)(2,1)} %param.6) | copy-start | bytes 743428
  2.7 15.2 %copy-start.2 = (bf16[88,1408]{1,0:T(8,128)(2,1)S(1)}, bf16[88,1408]{1,0:T(8,128)(2,1)}, u32[]{:S(2)}) copy-start(bf16[88,1408]{1,0:T(8,128)(2,1)} %param.7) | copy-start | bytes 743428
  2.7 11.1 %all-to-all-start = ((bf16[88,4,352]{2,0,1:T(8,128)(2,1)}), bf16[88,4,352]{2,0,1:T(8,128)(2,1)}, u32[]{:S(2)}, u32[]{:S(2)}) async-start(bf16[88,4,352]{2,0,1:T(8,128)(2,1)} %copy.33), calls=%async_computation | async-start | bytes 540672 | tf_op jit(solution)/shard_map/all_to_all | solution.py:33
  8.1 20.0 %copy-start.1 = (bf16[88,1408]{1,0:T(8,128)(2,1)S(1)}, bf16[88,1408]{1,0:T(8,128)(2,1)}, u32[]{:S(2)}) copy-start(bf16[88,1408]{1,0:T(8,128)(2,1)} %param.5) | copy-start | bytes 743428
  13.7 10.3 %all-to-all-start.3 = ((bf16[88,4,352]{2,0,1:T(8,128)(2,1)}), bf16[88,4,352]{2,0,1:T(8,128)(2,1)}, u32[]{:S(2)}, u32[]{:S(2)}) async-start(bf16[88,4,352]{2,0,1:T(8,128)(2,1)} %copy.37), calls=%async_computation.3 | async-start | bytes 540672 | tf_op jit(solution)/shard_map/all_to_all | solution.py:34
  18.1 20.0 %copy-start.4 = (f32[1408]{0:T(1024)S(1)}, f32[1408]{0:T(1024)}, u32[]{:S(2)}) copy-start(f32[1408]{0:T(1024)} %param.9) | copy-start | bytes 16900
  24.0 10.2 %all-to-all-start.6 = ((bf16[88,4,352]{2,0,1:T(8,128)(2,1)}), bf16[88,4,352]{2,0,1:T(8,128)(2,1)}, u32[]{:S(2)}, u32[]{:S(2)}) async-start(bf16[88,4,352]{2,0,1:T(8,128)(2,1)} %copy.41), calls=%async_computation.6 | async-start | bytes 540672 | tf_op jit(solution)/shard_map/all_to_all | solution.py:35
  34.2 9.3 %all-to-all-start.1 = ((bf16[2,2,88,352]{3,2,1,0:T(8,128)(2,1)}), bf16[2,2,88,352]{3,2,1,0:T(8,128)(2,1)S(1)}, u32[]{:S(2)}, u32[]{:S(2)}) async-start(bf16[2,2,88,352]{3,2,1,0:T(8,128)(2,1)} %bitcast.1), calls=%async_computation.1 | async-start | bytes 540672 | tf_op jit(solution)/shard_map/all_to_all | solution.py:42
  43.5 8.7 %all-to-all-start.4 = ((bf16[2,2,88,352]{3,2,1,0:T(8,128)(2,1)}), bf16[2,2,88,352]{3,2,1,0:T(8,128)(2,1)S(1)}, u32[]{:S(2)}, u32[]{:S(2)}) async-start(bf16[2,2,88,352]{3,2,1,0:T(8,128)(2,1)} %bitcast.8), calls=%async_computation.4 | async-start | bytes 540672 | tf_op jit(solution)/shard_map/all_to_all | solution.py:42
  52.1 8.7 %all-to-all-start.7 = ((bf16[2,2,88,352]{3,2,1,0:T(8,128)(2,1)}), bf16[2,2,88,352]{3,2,1,0:T(8,128)(2,1)S(1)}, u32[]{:S(2)}, u32[]{:S(2)}) async-start(bf16[2,2,88,352]{3,2,1,0:T(8,128)(2,1)} %bitcast.15), calls=%async_computation.7 | async-start | bytes 540672 | tf_op jit(solution)/shard_map/all_to_all | solution.py:42
  60.8 53.9 %all-to-all-start.2 = ((bf16[4,1,1,88,352]{4,3,2,1,0:T(8,128)(2,1)}), bf16[4,1,1,88,352]{4,3,2,1,0:T(8,128)(2,1)S(1)}, u32[]{:S(2)}, u32[]{:S(2)}) async-start(bf16[4,1,1,88,352]{4,3,2,1,0:T(8,128)(2,1)} %bitcast.5), calls=%async_computation.2 | async-start | bytes 540672 | tf_op jit(solution)/shard_map/all_to_all | solution.py:50
  114.7 14.7 %all-to-all-start.5 = ((bf16[4,1,1,88,352]{4,3,2,1,0:T(8,128)(2,1)}), bf16[4,1,1,88,352]{4,3,2,1,0:T(8,128)(2,1)S(1)}, u32[]{:S(2)}, u32[]{:S(2)}) async-start(bf16[4,1,1,88,352]{4,3,2,1,0:T(8,128)(2,1)} %bitcast.12), calls=%async_computation.5 | async-start | bytes 540672 | tf_op jit(solution)/shard_map/all_to_all | solution.py:50
  129.4 17.4 %all-to-all-start.8 = ((bf16[4,1,1,88,352]{4,3,2,1,0:T(8,128)(2,1)}), bf16[4,1,1,88,352]{4,3,2,1,0:T(8,128)(2,1)S(1)}, u32[]{:S(2)}, u32[]{:S(2)}) async-start(bf16[4,1,1,88,352]{4,3,2,1,0:T(8,128)(2,1)} %bitcast.19), calls=%async_computation.8 | async-start | bytes 540672 | tf_op jit(solution)/shard_map/all_to_all | solution.py:50
